TPU v7x, 128 devices: a whole 4x4x4 slice. The times are simulated.
128 devices in a mesh: tp: 4 (over z), dp: 4 (over y), pp: 8 (over x, core).
Axes of the slice: x: 4, y: 4, z: 4, core: 2. Of those that a mesh axis runs over, the one named last changes fastest.
Arguments:
- master: float32 [50304, 768], P('tp')
- exp_avg: float32 [50304, 768], P('tp')
- exp_avg_sq: float32 [50304, 768], P('tp')
- stage_ids: int32 [8, 24, 384], P('pp', 'dp')
- stage_acts: bfloat16 [8, 24, 384, 768], P('pp', 'dp')
Outputs:
- output 1: float32 [50304, 768], P('tp')
- output 2: float32 [50304, 768], P('tp')
- output 3: float32 [50304, 768], P('tp')
- output 4: bfloat16 [50304, 768], P('tp')
All inputs are finite; a program needn't handle non-finite values.
Results may differ from a plain program's by a relative error of at most 0.001.
Values sent between devices are 32-bit elements.
A program may use at most 1 GiB of HBM per device.

v0:
```python
import jax
import jax.numpy as jnp
from jax import lax
from jax.sharding import PartitionSpec as P

LEARN_RATE = 0.003
BETA_ONE = 0.9
BETA_TWO = 0.95
ADAM_EPS = 1e-8
WEIGHT_DECAY = 0.1
CLIP_NORM = 1.0
OPT_STEP = 10


def stage_grad(master_blk, tok_ids, tok_acts, n_stage):
    stage_idx = lax.axis_index("pp")
    vocab_dev, model_dim = master_blk.shape
    tok_count = tok_ids.shape[1] * tok_ids.shape[2]
    tok_flat = tok_ids.reshape(tok_count)
    act_flat = tok_acts.reshape(tok_count, model_dim)
    row_ids = lax.axis_index("tp") * vocab_dev + lax.broadcasted_iota(jnp.int32, (1, vocab_dev), 1)
    hit_mask = tok_flat[:, None] == row_ids
    logits = jnp.einsum("td,vd->tv", act_flat, master_blk.astype(jnp.bfloat16), preferred_element_type=jnp.float32)
    row_max = lax.pmax(jnp.max(logits, axis=1), "tp")
    exp_logits = jnp.exp(logits - row_max[:, None])
    row_sum = lax.psum(jnp.sum(exp_logits, axis=1), "tp")
    prob_mat = exp_logits / row_sum[:, None]
    dlogits = (jnp.where(hit_mask, prob_mat - 1.0, prob_mat) / tok_count).astype(jnp.bfloat16)
    coeff_mat = jnp.where(stage_idx == 0, hit_mask.astype(jnp.bfloat16), dlogits)
    contrib = jnp.einsum("tv,td->vd", coeff_mat, act_flat, preferred_element_type=jnp.float32)
    active = jnp.logical_or(stage_idx == 0, stage_idx == n_stage - 1)
    return jnp.where(active, contrib, 0.0)


def adamw_update(master, exp_avg, exp_avg_sq, gradient):
    sq_total = lax.psum(jnp.sum(gradient * gradient), "tp")
    gradient = gradient * (CLIP_NORM / jnp.maximum(jnp.sqrt(sq_total), CLIP_NORM))
    new_avg = BETA_ONE * exp_avg + (1.0 - BETA_ONE) * gradient
    new_avg_sq = BETA_TWO * exp_avg_sq + (1.0 - BETA_TWO) * gradient * gradient
    step_dir = (new_avg / (1.0 - BETA_ONE ** OPT_STEP)) / (jnp.sqrt(new_avg_sq / (1.0 - BETA_TWO ** OPT_STEP)) + ADAM_EPS)
    new_master = master - LEARN_RATE * (step_dir + WEIGHT_DECAY * master)
    return new_master, new_avg, new_avg_sq, new_master.astype(jnp.bfloat16)


def solution(mesh):
    n_stage = mesh.shape["pp"]
    n_repl = mesh.shape["dp"]
    table_spec = P("tp", None)

    def device_step(master, exp_avg, exp_avg_sq, stage_ids, stage_acts):
        contrib = stage_grad(master, stage_ids, stage_acts, n_stage)
        stage_sum = lax.psum(contrib, "pp")
        gradient = lax.psum(stage_sum, "dp") / n_repl
        return adamw_update(master, exp_avg, exp_avg_sq, gradient)

    return jax.shard_map(device_step, mesh=mesh, in_specs=(table_spec, table_spec, table_spec, P("pp", "dp", None), P("pp", "dp", None, None)), out_specs=(table_spec, table_spec, table_spec, table_spec), check_vma=False)
```

profile of v0, /device:TPU:1, one launch (start us, length us, event | category | flops | bytes accessed | tf_op | source)
XLA Modules:
  0.0 1382.5 jit_solution(12434302804724090761)
XLA Ops:
  7.2 0.0 copy-start
  7.2 0.0 all-reduce.3.cloned.1.call-start
  7.2 0.9 reduce
  8.1 0.6 eq.24
  8.7 0.6 iota_add_fusion
  9.3 0.0 copy-done
  9.4 60.0 %fusion.16 = (f32[2304]{0:T(1024)}, f32[2304,12576]{0,1:T(8,128)}) fusion(bf16[2304,768]{1,0:T(8,128)(2,1)S(1)} %bitcast.5, f32[12576,768]{1,0:T(8,128)} %param.5), kind=kOutput, calls=%fused_computation.20 | convolution fusion | flops 44544389120 | bytes 158082048 | tf_op jit(solution)/shard_map/td,vd->tv/dot_general | solution.py:23
  69.3 15.9 %pmax.7 = f32[2304]{0:T(1024)S(1)} all-reduce(f32[2304]{0:T(1024)} %get-tuple-element.8), channel_id=1, replica_groups=mesh['tp'=4,'dp'=4,'pp'=8] {'tp'}, use_global_device_ids=true, to_apply=%region_1.0 | all-reduce | flops 2304 | bytes 18432 | tf_op jit(solution)/shard_map/pmax | solution.py:24
  85.2 36.0 %fusion.2 = f32[2304]{0:T(1024)} fusion(f32[2304,12576]{0,1:T(8,128)} %get-tuple-element.9, f32[2304]{0:T(1024)S(1)} %pmax.7), kind=kLoop, calls=%fused_computation.5 | loop fusion | flops 57947904 | bytes 115918848 | tf_op jit(solution)/shard_map/reduce_sum | solution.py:26
  121.2 12.3 psum.28
  133.5 80.2 %fusion.7 = f32[12576,768]{1,0:T(8,128)} fusion(bf16[2304,768]{1,0:T(8,128)(2,1)S(1)} %bitcast.6, f32[2304,12576]{0,1:T(8,128)} %get-tuple-element.9, f32[2304]{0:T(1024)} %psum.28, f32[2304]{0:T(1024)S(1)} %pmax.7, s32[2304]{0:T(1024)} %eq.24, s32[12576]{0:T(1024)} %iota_add_fusion, pred[]{:T(512)S(6)} %eq.22, pred[]{:T(512)S(6)} %or.3), kind=kOutput, calls=%fused_computation.13 | convolution fusion | flops 44776194048 | bytes 158150784 | tf_op jit(solution)/shard_map/tv,td->vd/dot_general | solution.py:30
  213.8 0.0 all-reduce.3.cloned.1.call-update
  213.8 0.0 all-reduce.5.cloned.1.call-start
  213.8 394.2 %all-reduce.3.cloned.1.call-done = f32[12576,768]{1,0:T(8,128)} async-done(((f32[12576,768]{1,0:T(8,128)}), f32[12576,768]{1,0:T(8,128)}) %all-reduce.3.cloned.1.call-update) | async-done | bytes 38633488 | tf_op jit(solution)/shard_map/psum | solution.py:52
  608.0 0.0 all-reduce.5.cloned.1.call-update
  608.0 649.3 %all-reduce.5.cloned.1.call-done = f32[12576,768]{1,0:T(8,128)} async-done(((f32[12576,768]{1,0:T(8,128)}), f32[12576,768]{1,0:T(8,128)}) %all-reduce.5.cloned.1.call-update) | async-done | bytes 38633488 | tf_op jit(solution)/shard_map/psum | solution.py:53
  1257.3 17.6 %multiply_reduce_fusion = f32[]{:T(128)} fusion(f32[12576,768]{1,0:T(8,128)} %all-reduce.5.cloned.1.call-done), kind=kLoop, calls=%fused_computation.12 | loop fusion | flops 28975104 | bytes 38633476 | tf_op jit(solution)/shard_map/reduce_sum | solution.py:36
  1274.9 9.5 psum.31
  1285.1 0.0 copy-start.1
  1285.1 90.5 %fusion.14 = (bf16[12576,768]{1,0:T(8,128)(2,1)}, f32[12576,768]{1,0:T(8,128)}, f32[12576,768]{1,0:T(8,128)}, f32[12576,768]{1,0:T(8,128)}) fusion(f32[12576,768]{1,0:T(8,128)} %param.5, f32[12576,768]{1,0:T(8,128)} %all-reduce.5.cloned.1.call-done, f32[]{:T(128)S(6)} %mul.51, f32[12576,768]{1,0:T(8,128)} %param.6, f32[12576,768]{1,0:T(8,128)} %param.7), kind=kLoop, calls=%fused_computation.19 | loop fusion | flops 164192256 | bytes 289751040 | tf_op jit(solution)/shard_map/convert_element_type | solution.py:42
  1375.6 0.0 copy-done.1
Async XLA Ops:
  7.2 2.2 copy-start
  7.2 600.8 %all-reduce.3.cloned.1.call-start = ((), (), s32[]{:S(2)}) async-start(), calls=%async_computation | async-start | bytes 77266944 | tf_op jit(solution)/shard_map/psum | solution.py:52
  213.8 1043.5 %all-reduce.5.cloned.1.call-start = ((), (), s32[]{:S(2)}) async-start(), calls=%async_computation.1 | async-start | bytes 77266944 | tf_op jit(solution)/shard_map/psum | solution.py:53
  1285.1 90.5 %copy-start.1 = (bf16[1,6,384,768]{3,2,1,0:T(8,128)(2,1)S(1)}, bf16[1,6,384,768]{3,2,1,0:T(8,128)(2,1)}, u32[]{:S(2)}) copy-start(bf16[1,6,384,768]{3,2,1,0:T(8,128)(2,1)} %param.9) | copy-start | bytes 10616836
Sparse Core Ops, SparseCore 0:
  213.9 394.0 all-reduce.2
  610.5 646.7 all-reduce.4
where the time goes:
time: 1380 us
  waiting for transfers between devices  1040 us (75%)
  other arithmetic  146 us (11%)
  matrix products  140 us (10%)
  blocking collectives  37.7 us (3%)
  between operations  14.8 us (1%)
    psum x1, waiting for transfers between devices, device_step(): gradient = lax.psum(stage_sum, 'dp') / n_repl  649 us
    psum x1, waiting for transfers between devices, device_step(): stage_sum = lax.psum(contrib, 'pp')  394 us
    convert_element_type x1, other arithmetic, adamw_update(): return (new_master, new_avg, new_avg_sq, new_master.astype(jnp.bfloat16))  90.5 us
    dot_general x1, matrix products, stage_grad(): jnp.einsum('tv,td->vd', coeff_mat, act_flat, preferred_element_type=jnp.f...  80.2 us
    dot_general x1, matrix products, stage_grad(): jnp.einsum('td,vd->tv', act_flat, master_blk.astype(jnp.bfloat16), prefer...  60 us
    reduce_sum x1, other arithmetic, stage_grad(): row_sum = lax.psum(jnp.sum(exp_logits, axis=1), 'tp')  36 us
  transfers between devices with their start and end apart: 2, of which 2 were waited for; matrix products, arithmetic and copies ran while one was open for 0% of the time, Pallas kernels for 0%

commit v1 on v0

v1 whole, which is shorter than its diff:
```python
import functools

import jax
import jax.numpy as jnp
from jax import lax
from jax.experimental import pallas as pl
from jax.experimental.pallas import tpu as pltpu
from jax.sharding import PartitionSpec as P

LEARN_RATE = 0.003
BETA_ONE = 0.9
BETA_TWO = 0.95
ADAM_EPS = 1e-8
WEIGHT_DECAY = 0.1
CLIP_NORM = 1.0
OPT_STEP = 10

MESH = pl.DeviceIdType.MESH
ANY = pl.BlockSpec(memory_space=pl.ANY)
VMEM = pl.BlockSpec(memory_space=pltpu.VMEM)
NEG_BIG = float("-inf")


def barrier_with(axis_sizes):
    barrier = pltpu.get_barrier_semaphore()
    total = 0
    for axis, size in axis_sizes:
        me = lax.axis_index(axis)
        for k in range(1, size):
            pl.semaphore_signal(barrier, inc=1, device_id={axis: lax.rem(me + k, size)}, device_id_type=MESH)
            total += 1
    pl.semaphore_wait(barrier, total)


def in_block(local, block_rows):
    return jnp.where(local < block_rows, local, -(2**30))


def scatter_kernel(n_pp, n_tp, acts, toks, hid_out, dx_out, lab_out, ids_out, stage_bf, stage_f, tok_vm, load_sem, send_sem, recv_sem):
    me = lax.axis_index("pp")
    quarter = stage_f.shape[0]
    piece = quarter // n_pp
    sources = ((0, 0, dx_out, ids_out), (1, n_pp - 1, hid_out, lab_out))
    start = pl.multiple_of(lax.axis_index("tp") * quarter, quarter)
    load_a = pltpu.make_async_copy(acts.at[pl.ds(start, quarter), :], stage_bf, load_sem.at[0])
    load_t = pltpu.make_async_copy(toks, tok_vm, load_sem.at[1])
    load_a.start()
    load_t.start()
    load_a.wait()
    load_t.wait()
    stage_f[...] = stage_bf[...].astype(jnp.float32)
    barrier_with((("pp", n_pp),))
    for which, src, act_out, tok_out in sources:

        def copies(dest, which=which, act_out=act_out, tok_out=tok_out):
            a = pltpu.make_async_remote_copy(
                src_ref=stage_f.at[pl.ds(dest * piece, piece), :],
                dst_ref=act_out,
                send_sem=send_sem.at[which, 0, dest],
                recv_sem=recv_sem.at[which, 0],
                device_id={"pp": dest},
                device_id_type=MESH,
            )
            t = pltpu.make_async_remote_copy(
                src_ref=tok_vm,
                dst_ref=tok_out,
                send_sem=send_sem.at[which, 1, dest],
                recv_sem=recv_sem.at[which, 1],
                device_id={"pp": dest},
                device_id_type=MESH,
            )
            return a, t

        @pl.when(me == src)
        def _(src=src, which=which, act_out=act_out, tok_out=tok_out, copies=copies):
            for dest in range(n_pp):
                if dest != src:
                    for c in copies(dest):
                        c.start()
            own_a = pltpu.make_async_copy(stage_f.at[pl.ds(src * piece, piece), :], act_out, load_sem.at[0])
            own_t = pltpu.make_async_copy(tok_vm, tok_out, load_sem.at[1])
            own_a.start()
            own_t.start()
            own_a.wait()
            own_t.wait()

    for which, src, act_out, tok_out in sources:

        def waits(dest, which=which, act_out=act_out, tok_out=tok_out):
            a = pltpu.make_async_remote_copy(
                src_ref=stage_f.at[pl.ds(dest * piece, piece), :],
                dst_ref=act_out,
                send_sem=send_sem.at[which, 0, dest],
                recv_sem=recv_sem.at[which, 0],
                device_id={"pp": dest},
                device_id_type=MESH,
            )
            t = pltpu.make_async_remote_copy(
                src_ref=tok_vm,
                dst_ref=tok_out,
                send_sem=send_sem.at[which, 1, dest],
                recv_sem=recv_sem.at[which, 1],
                device_id={"pp": dest},
                device_id_type=MESH,
            )
            return a, t

        @pl.when(me == src)
        def _(src=src, waits=waits):
            for dest in range(n_pp):
                if dest != src:
                    for c in waits(dest):
                        c.wait_send()

        @pl.when(me != src)
        def _(src=src, waits=waits):
            other = (src + 1) % n_pp
            for c in waits(other):
                c.wait_recv()


def scatter_sources(acts, toks, n_pp, n_tp):
    tok_count, dim = acts.shape
    quarter = tok_count // n_tp
    piece = quarter // n_pp
    return pl.pallas_call(
        functools.partial(scatter_kernel, n_pp, n_tp),
        out_shape=(
            jax.ShapeDtypeStruct((piece, dim), jnp.float32),
            jax.ShapeDtypeStruct((piece, dim), jnp.float32),
            jax.ShapeDtypeStruct((1, tok_count), jnp.int32),
            jax.ShapeDtypeStruct((1, tok_count), jnp.int32),
        ),
        in_specs=[ANY, ANY],
        out_specs=(ANY, ANY, ANY, ANY),
        scratch_shapes=[
            pltpu.VMEM((quarter, dim), jnp.bfloat16),
            pltpu.VMEM((quarter, dim), jnp.float32),
            pltpu.VMEM((1, tok_count), jnp.int32),
            pltpu.SemaphoreType.DMA((2,)),
            pltpu.SemaphoreType.DMA((2, 2, n_pp)),
            pltpu.SemaphoreType.DMA((2, 2)),
        ],
        compiler_params=pltpu.CompilerParams(collective_id=1, has_side_effects=True),
        name="scatter_sources",
    )(acts, toks)


def dlogits_kernel(
    lay, n_pp, n_tp, block_rows, master, hid, lab, dlog_out, hid_bf_out, e_f, e_bf, h_f, h_bf, logit, dlog, lse, gath_a, gath_b, e_sem, h_sem, out_sem, send_sem, recv_sem
):
    me = lax.axis_index("pp")
    tpi = lax.axis_index("tp")
    chunks, n_dp, piece = lay
    rows_chunk = n_dp * piece
    tok_count, dim = h_f.shape
    tok_tile = min(256, tok_count)
    n_tile = tok_count // tok_tile
    span = n_dp * n_pp * piece
    tail = block_rows % piece

    def first_row(c, d):
        return c * span + (d * n_pp + me) * piece

    def hid_copy(t):
        at = pl.ds(pl.multiple_of(t * tok_tile, tok_tile), tok_tile)
        return pltpu.make_async_copy(hid.at[at, :], h_f.at[at, :], h_sem.at[t])

    def row_copy(c, d, n):
        slot = c * rows_chunk + d * piece
        start = pl.multiple_of(first_row(c, d), 8)
        return pltpu.make_async_copy(master.at[pl.ds(start, n), :], e_f.at[pl.ds(slot, n), :], e_sem.at[c])

    def on_rows(act):
        for c in range(chunks):
            for d in range(n_dp):
                if c * span + (d * n_pp + n_pp - 1) * piece + piece <= block_rows:
                    act(row_copy(c, d, piece))
                else:

                    @pl.when(first_row(c, d) + piece <= block_rows)
                    def _(c=c, d=d):
                        act(row_copy(c, d, piece))

                    if tail:

                        @pl.when(first_row(c, d) + tail == block_rows)
                        def _(c=c, d=d):
                            act(row_copy(c, d, tail))

    on_rows(lambda c: c.start())
    for t in range(n_tile):
        hid_copy(t).start()
    barrier_with((("pp", n_pp), ("tp", n_tp)))
    on_rows(lambda c: c.wait())

    iota_p = lax.broadcasted_iota(jnp.int32, (piece, tok_tile), 0)
    for c in range(chunks):
        for d in range(n_dp):
            at = pl.ds(c * rows_chunk + d * piece, piece)
            rows = e_f[at, :]
            if c * span + (d * n_pp + n_pp - 1) * piece + piece > block_rows:
                inside = lax.broadcasted_iota(jnp.int32, (piece, dim), 0) + first_row(c, d) < block_rows
                rows = jnp.where(inside, rows, 0.0)
            e_bf[at, :] = rows.astype(jnp.bfloat16)

    def logit_tile(t, _):
        at = pl.ds(pl.multiple_of(t * tok_tile, tok_tile), tok_tile)
        hid_copy(t).wait()
        h_tile = h_f[at, :].astype(jnp.bfloat16)
        h_bf[at, :] = h_tile
        top = jnp.full((8, tok_tile), NEG_BIG, jnp.float32)
        for c in range(chunks):
            rows = pl.ds(c * rows_chunk, rows_chunk)
            val = lax.dot_general(e_bf[rows, :], h_tile, (((1,), (1,)), ((), ())), preferred_element_type=jnp.float32)
            for d in range(n_dp):
                part = val[d * piece : (d + 1) * piece]
                if c * span + (d * n_pp + n_pp - 1) * piece + piece > block_rows:
                    part = jnp.where(iota_p + first_row(c, d) < block_rows, part, NEG_BIG)
                logit[pl.ds(c * rows_chunk + d * piece, piece), at] = part
                top = jnp.maximum(top, jnp.max(part.reshape(piece // 8, 8, tok_tile), axis=0))
        top = jnp.max(top, axis=0, keepdims=True)
        total = jnp.zeros((8, tok_tile), jnp.float32)
        for c in range(chunks):
            val = jnp.exp(logit[pl.ds(c * rows_chunk, rows_chunk), at] - top)
            total = total + jnp.sum(val.reshape(rows_chunk // 8, 8, tok_tile), axis=0)
        lse[:, at] = top + jnp.log(jnp.sum(total, axis=0, keepdims=True))
        return 0

    lax.fori_loop(0, n_tile, logit_tile, 0)
    hid_bf_copy = pltpu.make_async_copy(h_bf, hid_bf_out, out_sem.at[chunks])
    hid_bf_copy.start()

    def exchange(axis, size, gathered, stage):
        idx = lax.axis_index(axis)
        sends = []
        for k in range(1, size):
            copy = pltpu.make_async_remote_copy(
                src_ref=lse,
                dst_ref=gathered.at[k],
                send_sem=send_sem.at[stage, k],
                recv_sem=recv_sem.at[stage, k],
                device_id={axis: lax.rem(idx + k, size)},
                device_id_type=MESH,
            )
            copy.start()
            sends.append(copy)
        own = lse[...]
        for copy in sends:
            copy.wait()
        top = own
        for k in range(1, size):
            top = jnp.maximum(top, gathered[k])
        total = jnp.exp(own - top)
        for k in range(1, size):
            total = total + jnp.exp(gathered[k] - top)
        lse[...] = top + jnp.log(total)

    exchange("pp", n_pp, gath_a, 0)
    exchange("tp", n_tp, gath_b, 1)

    inv_tok = 1.0 / tok_count
    vocab_base = tpi * block_rows

    for c in range(chunks):

        def dlog_tile(t, _, c=c):
            at = pl.ds(pl.multiple_of(t * tok_tile, tok_tile), tok_tile)
            norm = lse[:, at]
            labels = in_block(lab[:, at] - vocab_base, block_rows)
            for d in range(n_dp):
                rows = pl.ds(c * rows_chunk + d * piece, piece)
                prob = jnp.exp(logit[rows, at] - norm)
                hit = iota_p == labels - first_row(c, d)
                dlog[rows, at] = (jnp.where(hit, prob - 1.0, prob) * inv_tok).astype(jnp.bfloat16)
            return 0

        lax.fori_loop(0, n_tile, dlog_tile, 0)
        rows = pl.ds(c * rows_chunk, rows_chunk)
        pltpu.make_async_copy(dlog.at[rows, :], dlog_out.at[rows, :], out_sem.at[c]).start()
    for c in range(chunks):
        rows = pl.ds(c * rows_chunk, rows_chunk)
        pltpu.make_async_copy(dlog.at[rows, :], dlog_out.at[rows, :], out_sem.at[c]).wait()
    hid_bf_copy.wait()


def head_dlogits(master, hid, lab, lay, n_pp, n_tp):
    chunks, n_dp, piece = lay
    rows = chunks * n_dp * piece
    tok_count, dim = hid.shape
    n_tile = tok_count // min(256, tok_count)
    return pl.pallas_call(
        functools.partial(dlogits_kernel, lay, n_pp, n_tp, master.shape[0]),
        out_shape=(jax.ShapeDtypeStruct((rows, tok_count), jnp.bfloat16), jax.ShapeDtypeStruct((tok_count, dim), jnp.bfloat16)),
        in_specs=[ANY, ANY, VMEM],
        out_specs=(ANY, ANY),
        scratch_shapes=[
            pltpu.VMEM((rows, dim), jnp.float32),
            pltpu.VMEM((rows, dim), jnp.bfloat16),
            pltpu.VMEM((tok_count, dim), jnp.float32),
            pltpu.VMEM((tok_count, dim), jnp.bfloat16),
            pltpu.VMEM((rows, tok_count), jnp.float32),
            pltpu.VMEM((rows, tok_count), jnp.bfloat16),
            pltpu.VMEM((1, tok_count), jnp.float32),
            pltpu.VMEM((n_pp, 1, tok_count), jnp.float32),
            pltpu.VMEM((n_tp, 1, tok_count), jnp.float32),
            pltpu.SemaphoreType.DMA((chunks,)),
            pltpu.SemaphoreType.DMA((n_tile,)),
            pltpu.SemaphoreType.DMA((chunks + 1,)),
            pltpu.SemaphoreType.DMA((2, n_pp)),
            pltpu.SemaphoreType.DMA((2, n_pp)),
        ],
        compiler_params=pltpu.CompilerParams(collective_id=2, has_side_effects=True, vmem_limit_bytes=58 * 2**20),
        cost_estimate=pl.CostEstimate(flops=20 * 10**9, bytes_accessed=25 * 10**6, transcendentals=8 * 10**6),
        name="head_dlogits",
    )(master, hid, lab)


def grad_kernel(chunk, lay, n_pp, block_rows, dlog, hid_bf, dx, ids, out):
    chunks, n_dp, piece = lay
    t = pl.program_id(0)
    me = lax.axis_index("pp")
    tok = in_block(ids[...] - lax.axis_index("tp") * block_rows, block_rows)
    tok = tok - (chunk * n_dp * n_pp * piece + me * piece)
    iota_p = lax.broadcasted_iota(jnp.int32, (piece, ids.shape[1]), 0)
    one_hot = jnp.concatenate(
        [jnp.where(iota_p == tok - d * n_pp * piece, 1.0, 0.0).astype(jnp.bfloat16) for d in range(n_dp)], axis=0
    )
    val = jnp.dot(dlog[...], hid_bf[...], preferred_element_type=jnp.float32)
    val = val + jnp.dot(one_hot, dx[...].astype(jnp.bfloat16), preferred_element_type=jnp.float32)

    @pl.when(t == 0)
    def _():
        out[...] = val

    @pl.when(t != 0)
    def _():
        out[...] += val


def chunk_grad(dlog, hid_bf, dx, ids, chunk, lay, n_pp, block_rows):
    chunks, n_dp, piece = lay
    rows = n_dp * piece
    tok_count, dim = hid_bf.shape
    tile = min(256, tok_count)
    return pl.pallas_call(
        functools.partial(grad_kernel, chunk, lay, n_pp, block_rows),
        grid=(tok_count // tile,),
        out_shape=jax.ShapeDtypeStruct((rows, dim), jnp.float32),
        in_specs=[
            pl.BlockSpec((rows, tile), lambda t: (chunk, t)),
            pl.BlockSpec((tile, dim), lambda t: (t, 0)),
            pl.BlockSpec((tile, dim), lambda t: (t, 0)),
            pl.BlockSpec((1, tile), lambda t: (0, t)),
        ],
        out_specs=pl.BlockSpec((rows, dim), lambda t: (0, 0)),
        cost_estimate=pl.CostEstimate(flops=3 * 10**9, bytes_accessed=13 * 10**6, transcendentals=0),
        name=f"grad_{chunk}",
    )(dlog, hid_bf, dx, ids)


def adamw_kernel(n_prev, factor, grad, master, avg, avg_sq, *refs):
    new_master, new_avg, new_sq, new_bf = refs[n_prev:]
    g = grad[...] * factor[0, 0]
    m = BETA_ONE * avg[...] + (1.0 - BETA_ONE) * g
    v = BETA_TWO * avg_sq[...] + (1.0 - BETA_TWO) * g * g
    step_dir = (m * (1.0 / (1.0 - BETA_ONE**OPT_STEP))) / (jnp.sqrt(v * (1.0 / (1.0 - BETA_TWO**OPT_STEP))) + ADAM_EPS)
    w = master[...]
    w = w - LEARN_RATE * (step_dir + WEIGHT_DECAY * w)
    new_master[...] = w
    new_avg[...] = m
    new_sq[...] = v
    new_bf[...] = w.astype(jnp.bfloat16)


def tile_of(rows, most):
    return max(t for t in range(8, most + 1, 8) if rows % t == 0)


def chunk_update(factor, grad, master, avg, avg_sq, prev, row0):
    dim = grad.shape[1]
    rows = min(grad.shape[0], master.shape[0] - row0)
    tile = tile_of(rows, 640)
    table = pl.BlockSpec((pl.Element(tile), pl.Element(dim)), lambda i: (pl.multiple_of(row0 + i * tile, 8), 0))
    grad_spec = pl.BlockSpec((pl.Element(tile), pl.Element(dim)), lambda i: (pl.multiple_of(i * tile, 8), 0))
    n_prev = len(prev)
    return pl.pallas_call(
        functools.partial(adamw_kernel, n_prev),
        grid=(rows // tile,),
        out_shape=(
            jax.ShapeDtypeStruct(master.shape, jnp.float32),
            jax.ShapeDtypeStruct(master.shape, jnp.float32),
            jax.ShapeDtypeStruct(master.shape, jnp.float32),
            jax.ShapeDtypeStruct(master.shape, jnp.bfloat16),
        ),
        in_specs=[pl.BlockSpec(memory_space=pltpu.SMEM), grad_spec, table, table, table] + [ANY] * n_prev,
        out_specs=(table, table, table, table),
        input_output_aliases={5 + i: i for i in range(n_prev)},
        cost_estimate=pl.CostEstimate(flops=10**10, bytes_accessed=rows * dim * 30, transcendentals=rows * dim),
        name=f"adamw_{row0}",
    )(factor, grad, master, avg, avg_sq, *prev)


def layout_of(block_rows, n_dp, n_pp):
    chunks = 5
    unit = chunks * n_dp * n_pp
    piece = -(-block_rows // unit)
    return chunks, n_dp, -(-piece // 16) * 16


def solution(mesh):
    n_tp, n_dp, n_pp = mesh.shape["tp"], mesh.shape["dp"], mesh.shape["pp"]
    table_spec = P("tp", None)

    def device_step(master, exp_avg, exp_avg_sq, stage_ids, stage_acts):
        block_rows, dim = master.shape
        lay = layout_of(block_rows, n_dp, n_pp)
        chunks, _, piece = lay
        tok_count = stage_ids.shape[1] * stage_ids.shape[2]
        toks = stage_ids.reshape(1, tok_count)
        acts = stage_acts.reshape(tok_count, dim)
        hid_piece, dx_piece, lab, ids = scatter_sources(acts, toks, n_pp, n_tp)
        hid = lax.all_gather(hid_piece, ("tp", "pp"), axis=0, tiled=True)
        dx = lax.all_gather(dx_piece, ("tp", "pp"), axis=0, tiled=True)
        dlog, hid_bf = head_dlogits(master, hid, lab, lay, n_pp, n_tp)
        shards = []
        for c in range(chunks):
            part = chunk_grad(dlog, hid_bf, dx, ids, c, lay, n_pp, block_rows)
            shards.append(lax.psum_scatter(part, "dp", scatter_dimension=0, tiled=True))
        sq_sum = sum(jnp.sum(s * s) for s in shards)
        sq_total = lax.psum(sq_sum, ("tp", "dp", "pp")) / (n_dp * n_dp)
        factor = (CLIP_NORM / jnp.maximum(jnp.sqrt(sq_total), CLIP_NORM)) / n_dp
        factor = factor.reshape(1, 1)
        outs = ()
        span = n_dp * n_pp * piece
        for c in range(chunks):
            grad = lax.all_gather(shards[c], ("dp", "pp"), axis=0, tiled=True)
            outs = tuple(chunk_update(factor, grad, master, exp_avg, exp_avg_sq, outs, c * span))
        return outs

    specs = (table_spec, table_spec, table_spec, P("pp", "dp", None), P("pp", "dp", None, None))
    return jax.shard_map(device_step, mesh=mesh, in_specs=specs, out_specs=(table_spec,) * 4, check_vma=False)
```

time: 1380 us -> 556 us (0.40)
  waiting for transfers between devices: 1040 us -> 274 us
  Pallas kernels: 0 us -> 187 us
  matrix products: 140 us -> 0 us
  other arithmetic: 146 us -> 8.06 us
  blocking collectives: 37.7 us -> 67.4 us
    psum x2 -> x0, waiting for transfers between devices: 1040 us -> none  [the longest x1 649 us: device_step(): gradient = lax.psum(stage_sum, 'dp') / n_repl]
    all_gather x0 -> x7, waiting for transfers between devices: none -> 191 us  [the longest x5 111 us: device_step(): grad = lax.all_gather(shards[c], ('dp', 'pp'), axis=0, tiled=True)]
    pallas_call x0 -> x12, Pallas kernels: none -> 187 us  [the longest x5 95.5 us: chunk_update(): pl.pallas_call(functools.partial(adamw_kernel, n_prev), grid=(rows // til...]
    dot_general x2 -> x0, matrix products: 140 us -> none  [the longest x1 80.2 us: stage_grad(): jnp.einsum('tv,td->vd', coeff_mat, act_flat, preferred_element_type=jnp.f...]
    convert_element_type x1 -> x0, other arithmetic: 90.5 us -> none  [adamw_update(): return (new_master, new_avg, new_avg_sq, new_master.astype(jnp.bfloat16))]
    reduce_scatter x0 -> x5, waiting for transfers between devices: none -> 81.2 us  [device_step(): shards.append(lax.psum_scatter(part, 'dp', scatter_dimension=0, tiled=True))]
    psum x2 -> x1, blocking collectives: 21.8 us -> 67.4 us  [device_step(): sq_total = lax.psum(sq_sum, ('tp', 'dp', 'pp')) / (n_dp * n_dp)]
    reduce_sum x2 -> x5, other arithmetic: 53.6 us -> 8.06 us  [device_step(): sq_sum = sum((jnp.sum(s * s) for s in shards))]
  transfers between devices with their start and end apart: 2 -> 12, of which waited for: 2 -> 10; matrix products, arithmetic and copies ran while one was open for 0% -> 1% of each run, Pallas kernels for 0% -> 26%
where the time goes in v1:
time: 556 us; the launch traced here: 555 us
  waiting for transfers between devices  274 us (49%)
  Pallas kernels  187 us (34%)
  blocking collectives  67.4 us (12%)
  between operations  18.2 us (3%)
  other arithmetic  8.06 us (1%)
    all_gather x5, waiting for transfers between devices, device_step(): grad = lax.all_gather(shards[c], ('dp', 'pp'), axis=0, tiled=True)  111 us
    pallas_call x5, Pallas kernels, chunk_update(): pl.pallas_call(functools.partial(adamw_kernel, n_prev), grid=(rows // til...  95.5 us
    reduce_scatter x5, waiting for transfers between devices, device_step(): shards.append(lax.psum_scatter(part, 'dp', scatter_dimension=0, tiled=True))  81.2 us
    psum x1, blocking collectives, device_step(): sq_total = lax.psum(sq_sum, ('tp', 'dp', 'pp')) / (n_dp * n_dp)  67.4 us
    all_gather x1, waiting for transfers between devices, device_step(): hid = lax.all_gather(hid_piece, ('tp', 'pp'), axis=0, tiled=True)  56.9 us
    pallas_call x5, Pallas kernels, chunk_grad(): pl.pallas_call(functools.partial(grad_kernel, chunk, lay, n_pp, block_row...  51.1 us
    pallas_call x1, Pallas kernels, head_dlogits(): pl.pallas_call(functools.partial(dlogits_kernel, lay, n_pp, n_tp, master....  27.6 us
    all_gather x1, waiting for transfers between devices, device_step(): dx = lax.all_gather(dx_piece, ('tp', 'pp'), axis=0, tiled=True)  23.9 us
  transfers between devices with their start and end apart: 12, of which 10 were waited for; matrix products, arithmetic and copies ran while one was open for 1% of the time, Pallas kernels for 26%

profile of v1, /device:TPU:1, one launch (start us, length us, event | category | flops | bytes accessed | tf_op | source)
XLA Modules:
  0.0 555.0 jit_solution(6769813570980671319)
XLA Ops:
  7.2 12.5 %scatter_sources.1 = (f32[72,768]{1,0:T(8,128)}, f32[72,768]{1,0:T(8,128)}, s32[1,2304]{1,0:T(1,128)}, s32[1,2304]{1,0:T(1,128)}) custom-call(bf16[2304,768]{1,0:T(8,128)(2,1)} %bitcast.3, s32[1,2304]{1,0:T(1,128)} %bitcast.4), custom_call_target="tpu_custom_call" | custom-call | tf_op jit(solution)/shard_map/scatter_sources/pallas_call | solution.py:126
  19.8 0.7 all-gather.10.cloned.1.call-update
  20.6 56.9 %all-gather.8.cloned.1.call-done.hid = f32[2304,768]{1,0:T(8,128)} async-done(((f32[72,768]{1,0:T(8,128)}), f32[2304,768]{1,0:T(8,128)}) %all-gather.8.cloned.1.call-update) | async-done | bytes 7077904 | tf_op jit(solution)/shard_map/all_gather | solution.py:423
  77.4 27.6 %head_dlogits.1 = (bf16[1600,2304]{1,0:T(8,128)(2,1)}, bf16[2304,768]{1,0:T(8,128)(2,1)}) custom-call(f32[12576,768]{1,0:T(8,128)} %master.11, f32[2304,768]{1,0:T(8,128)} %all-gather.8.cloned.1.call-done.hid, s32[1,2304]{1,0:T(1,128)} %get-tuple-element.27.lab), custom_call_target="tpu_custom_call" | custom-call | flops 20000000000 | bytes 25000000 | tf_op jit(solution)/shard_map/head_dlogits/pallas_call | solution.py:292
  105.0 23.9 %all-gather.10.cloned.1.call-done.dx = f32[2304,768]{1,0:T(8,128)} async-done(((f32[72,768]{1,0:T(8,128)}), f32[2304,768]{1,0:T(8,128)}) %all-gather.10.cloned.1.call-update) | async-done | bytes 7077904 | tf_op jit(solution)/shard_map/all_gather | solution.py:424
  128.9 10.2 %grad_0.1 = f32[320,768]{1,0:T(8,128)} custom-call(bf16[1600,2304]{1,0:T(8,128)(2,1)} %get-tuple-element.28.dlog, bf16[2304,768]{1,0:T(8,128)(2,1)} %get-tuple-element.29.hid_bf, f32[2304,768]{1,0:T(8,128)} %all-gather.10.cloned.1.call-done.dx, s32[1,2304]{1,0:T(1,128)} %get-tuple-element.31.ids), custom_call_target="tpu_custom_call" | custom-call | flops 3000000000 | bytes 13000000 | tf_op jit(solution)/shard_map/grad_0/pallas_call | solution.py:346
  139.2 10.2 %grad_1.1 = f32[320,768]{1,0:T(8,128)} custom-call(bf16[1600,2304]{1,0:T(8,128)(2,1)} %get-tuple-element.28.dlog, bf16[2304,768]{1,0:T(8,128)(2,1)} %get-tuple-element.29.hid_bf, f32[2304,768]{1,0:T(8,128)} %all-gather.10.cloned.1.call-done.dx, s32[1,2304]{1,0:T(1,128)} %get-tuple-element.31.ids), custom_call_target="tpu_custom_call" | custom-call | flops 3000000000 | bytes 13000000 | tf_op jit(solution)/shard_map/grad_1/pallas_call | solution.py:346
  149.4 0.0 reduce-scatter.10.cloned.1.call-start
  149.5 10.2 %grad_2.1 = f32[320,768]{1,0:T(8,128)} custom-call(bf16[1600,2304]{1,0:T(8,128)(2,1)} %get-tuple-element.28.dlog, bf16[2304,768]{1,0:T(8,128)(2,1)} %get-tuple-element.29.hid_bf, f32[2304,768]{1,0:T(8,128)} %all-gather.10.cloned.1.call-done.dx, s32[1,2304]{1,0:T(1,128)} %get-tuple-element.31.ids), custom_call_target="tpu_custom_call" | custom-call | flops 3000000000 | bytes 13000000 | tf_op jit(solution)/shard_map/grad_2/pallas_call | solution.py:346
  159.7 10.2 %grad_3.1 = f32[320,768]{1,0:T(8,128)} custom-call(bf16[1600,2304]{1,0:T(8,128)(2,1)} %get-tuple-element.28.dlog, bf16[2304,768]{1,0:T(8,128)(2,1)} %get-tuple-element.29.hid_bf, f32[2304,768]{1,0:T(8,128)} %all-gather.10.cloned.1.call-done.dx, s32[1,2304]{1,0:T(1,128)} %get-tuple-element.31.ids), custom_call_target="tpu_custom_call" | custom-call | flops 3000000000 | bytes 13000000 | tf_op jit(solution)/shard_map/grad_3/pallas_call | solution.py:346
  170.0 0.0 reduce-scatter.14.cloned.1.call-start
  170.0 10.2 %grad_4.1 = f32[320,768]{1,0:T(8,128)} custom-call(bf16[1600,2304]{1,0:T(8,128)(2,1)} %get-tuple-element.28.dlog, bf16[2304,768]{1,0:T(8,128)(2,1)} %get-tuple-element.29.hid_bf, f32[2304,768]{1,0:T(8,128)} %all-gather.10.cloned.1.call-done.dx, s32[1,2304]{1,0:T(1,128)} %get-tuple-element.31.ids), custom_call_target="tpu_custom_call" | custom-call | flops 3000000000 | bytes 13000000 | tf_op jit(solution)/shard_map/grad_4/pallas_call | solution.py:346
  180.4 0.7 all-gather.20.cloned.1.call-update
  181.1 3.9 reduce-scatter.8.cloned.1.call-done
  185.1 25.9 %reduce-scatter.10.cloned.1.call-done = f32[80,768]{1,0:T(8,128)} async-done(((f32[320,768]{1,0:T(8,128)}), f32[80,768]{1,0:T(8,128)}) %reduce-scatter.10.cloned.1.call-update) | async-done | bytes 245776 | tf_op jit(solution)/shard_map/reduce_scatter | solution.py:429
  211.1 25.9 %reduce-scatter.12.cloned.1.call-done = f32[80,768]{1,0:T(8,128)} async-done(((f32[320,768]{1,0:T(8,128)}), f32[80,768]{1,0:T(8,128)}) %reduce-scatter.12.cloned.1.call-update) | async-done | bytes 245776 | tf_op jit(solution)/shard_map/reduce_scatter | solution.py:429
  237.1 25.5 %reduce-scatter.14.cloned.1.call-done = f32[80,768]{1,0:T(8,128)} async-done(((f32[320,768]{1,0:T(8,128)}), f32[80,768]{1,0:T(8,128)}) %reduce-scatter.14.cloned.1.call-update) | async-done | bytes 245776 | tf_op jit(solution)/shard_map/reduce_scatter | solution.py:429
  262.6 1.6 multiply_reduce_fusion.3
  264.2 1.6 multiply_reduce_fusion.4
  267.1 1.6 multiply_reduce_fusion.2
  269.4 1.6 multiply_reduce_fusion.1
  271.6 1.6 multiply_reduce_fusion
  273.9 67.4 %psum.7 = f32[]{:T(128)} all-reduce(f32[]{:T(128)S(6)} %add.27), channel_id=1, replica_groups=mesh['tp'=4,'dp'=4,'pp'=8] {'tp','dp','pp'}, use_global_device_ids=true, to_apply=%region_10.0 | all-reduce | flops 1 | bytes 8 | tf_op jit(solution)/shard_map/psum | solution.py:431
  342.1 19.4 %adamw_0.1 = (f32[12576,768]{1,0:T(8,128)}, f32[12576,768]{1,0:T(8,128)}, f32[12576,768]{1,0:T(8,128)}, bf16[12576,768]{1,0:T(8,128)(2,1)}) custom-call(f32[1,1]{1,0:T(1,128)} %bitcast.2.factor, f32[2560,768]{1,0:T(8,128)} %all-gather.20.cloned.1.call-done.grad, f32[12576,768]{1,0:T(8,128)} %master.11, f32[12576,768]{1,0:T(8,128)} %avg.9, f32[12576,768]{1,0:T(8,128)} %avg_sq.9), custom_call_target="tpu_custom_call" | custom-call | flops 10000000000 | bytes 58982400 | tf_op jit(solution)/shard_map/adamw_0/pallas_call | solution.py:387
  361.5 10.1 %all-gather.18.cloned.1.call-done.grad = f32[2560,768]{1,0:T(8,128)} async-done(((f32[80,768]{1,0:T(8,128)}), f32[2560,768]{1,0:T(8,128)}) %all-gather.18.cloned.1.call-update) | async-done | bytes 7864336 | tf_op jit(solution)/shard_map/all_gather | solution.py:437
  371.5 19.4 %adamw_2560.1 = (f32[12576,768]{1,0:T(8,128)}, f32[12576,768]{1,0:T(8,128)}, f32[12576,768]{1,0:T(8,128)}, bf16[12576,768]{1,0:T(8,128)(2,1)}) custom-call(f32[1,1]{1,0:T(1,128)} %bitcast.2.factor, f32[2560,768]{1,0:T(8,128)} %all-gather.18.cloned.1.call-done.grad, ...), custom_call_target="tpu_custom_call", output_to_operand_aliasing={{0}: (5, {}), {1}: (6, {}), {2}: (7, {}), {3}: (8, {})} | custom-call | flops 10000000000 | bytes 58982400 | tf_op jit(solution)/shard_map/adamw_2560/pallas_call | solution.py:387
  390.9 33.5 %all-gather.16.cloned.1.call-done.grad = f32[2560,768]{1,0:T(8,128)} async-done(((f32[80,768]{1,0:T(8,128)}), f32[2560,768]{1,0:T(8,128)}) %all-gather.16.cloned.1.call-update) | async-done | bytes 7864336 | tf_op jit(solution)/shard_map/all_gather | solution.py:437
  424.4 19.4 %adamw_5120.1 = (f32[12576,768]{1,0:T(8,128)}, f32[12576,768]{1,0:T(8,128)}, f32[12576,768]{1,0:T(8,128)}, bf16[12576,768]{1,0:T(8,128)(2,1)}) custom-call(f32[1,1]{1,0:T(1,128)} %bitcast.2.factor, f32[2560,768]{1,0:T(8,128)} %all-gather.16.cloned.1.call-done.grad, ...), custom_call_target="tpu_custom_call", output_to_operand_aliasing={{0}: (5, {}), {1}: (6, {}), {2}: (7, {}), {3}: (8, {})} | custom-call | flops 10000000000 | bytes 58982400 | tf_op jit(solution)/shard_map/adamw_5120/pallas_call | solution.py:387
  443.8 33.6 %all-gather.14.cloned.1.call-done.grad = f32[2560,768]{1,0:T(8,128)} async-done(((f32[80,768]{1,0:T(8,128)}), f32[2560,768]{1,0:T(8,128)}) %all-gather.14.cloned.1.call-update) | async-done | bytes 7864336 | tf_op jit(solution)/shard_map/all_gather | solution.py:437
  477.4 19.4 %adamw_7680.1 = (f32[12576,768]{1,0:T(8,128)}, f32[12576,768]{1,0:T(8,128)}, f32[12576,768]{1,0:T(8,128)}, bf16[12576,768]{1,0:T(8,128)(2,1)}) custom-call(f32[1,1]{1,0:T(1,128)} %bitcast.2.factor, f32[2560,768]{1,0:T(8,128)} %all-gather.14.cloned.1.call-done.grad, ...), custom_call_target="tpu_custom_call", output_to_operand_aliasing={{0}: (5, {}), {1}: (6, {}), {2}: (7, {}), {3}: (8, {})} | custom-call | flops 10000000000 | bytes 58982400 | tf_op jit(solution)/shard_map/adamw_7680/pallas_call | solution.py:387
  496.8 33.5 %all-gather.12.cloned.1.call-done.grad = f32[2560,768]{1,0:T(8,128)} async-done(((f32[80,768]{1,0:T(8,128)}), f32[2560,768]{1,0:T(8,128)}) %all-gather.12.cloned.1.call-update) | async-done | bytes 7864336 | tf_op jit(solution)/shard_map/all_gather | solution.py:437
  530.3 17.9 %adamw_10240.1 = (f32[12576,768]{1,0:T(8,128)}, f32[12576,768]{1,0:T(8,128)}, f32[12576,768]{1,0:T(8,128)}, bf16[12576,768]{1,0:T(8,128)(2,1)}) custom-call(f32[1,1]{1,0:T(1,128)} %bitcast.2.factor, f32[2560,768]{1,0:T(8,128)} %all-gather.12.cloned.1.call-done.grad, ...), custom_call_target="tpu_custom_call", output_to_operand_aliasing={{0}: (5, {}), {1}: (6, {}), {2}: (7, {}), {3}: (8, {})} | custom-call | flops 10000000000 | bytes 53821440 | tf_op jit(solution)/shard_map/adamw_10240/pallas_call | solution.py:387
  (22 shorter events, 0.6 us)
Async XLA Ops:
  7.2 70.3 %all-gather.8.cloned.1.call-start = ((), (), s32[]{:S(2)}) async-start(), calls=%async_computation.5 | async-start | bytes 7299072 | tf_op jit(solution)/shard_map/all_gather | solution.py:423
  19.8 109.1 %all-gather.10.cloned.1.call-start = ((), (), s32[]{:S(2)}) async-start(), calls=%async_computation.6 | async-start | bytes 7299072 | tf_op jit(solution)/shard_map/all_gather | solution.py:424
  20.5 159.8 %reduce-scatter.6.cloned.1.call-start = ((), (), s32[]{:S(2)}) async-start(), calls=%async_computation.7 | async-start | bytes 1228800 | tf_op jit(solution)/shard_map/reduce_scatter | solution.py:429
  139.1 45.9 %reduce-scatter.8.cloned.1.call-start = ((), (), s32[]{:S(2)}) async-start(), calls=%async_computation.8 | async-start | bytes 1228800 | tf_op jit(solution)/shard_map/reduce_scatter | solution.py:429
  149.4 61.6 %reduce-scatter.10.cloned.1.call-start = ((), (), s32[]{:S(2)}) async-start(), calls=%async_computation.9 | async-start | bytes 1228800 | tf_op jit(solution)/shard_map/reduce_scatter | solution.py:429
  159.7 77.3 %reduce-scatter.12.cloned.1.call-start = ((), (), s32[]{:S(2)}) async-start(), calls=%async_computation.10 | async-start | bytes 1228800 | tf_op jit(solution)/shard_map/reduce_scatter | solution.py:429
  170.0 92.6 %reduce-scatter.14.cloned.1.call-start = ((), (), s32[]{:S(2)}) async-start(), calls=%async_computation.11 | async-start | bytes 1228800 | tf_op jit(solution)/shard_map/reduce_scatter | solution.py:429
  180.3 161.7 %all-gather.20.cloned.1.call-start = ((), (), s32[]{:S(2)}) async-start(), calls=%async_computation.16 | async-start | bytes 8110080 | tf_op jit(solution)/shard_map/all_gather | solution.py:437
  181.1 190.5 %all-gather.18.cloned.1.call-start = ((), (), s32[]{:S(2)}) async-start(), calls=%async_computation.15 | async-start | bytes 8110080 | tf_op jit(solution)/shard_map/all_gather | solution.py:437
  185.0 239.4 %all-gather.16.cloned.1.call-start = ((), (), s32[]{:S(2)}) async-start(), calls=%async_computation.14 | async-start | bytes 8110080 | tf_op jit(solution)/shard_map/all_gather | solution.py:437
  211.0 266.4 %all-gather.14.cloned.1.call-start = ((), (), s32[]{:S(2)}) async-start(), calls=%async_computation.13 | async-start | bytes 8110080 | tf_op jit(solution)/shard_map/all_gather | solution.py:437
  237.0 293.3 %all-gather.12.cloned.1.call-start = ((), (), s32[]{:S(2)}) async-start(), calls=%async_computation.12 | async-start | bytes 8110080 | tf_op jit(solution)/shard_map/all_gather | solution.py:437
Sparse Core Ops, SparseCore 0:
  19.9 57.4 all-gather.7
  79.7 49.1 all-gather.9
  139.2 19.7 reduce-scatter.5
  161.9 23.0 reduce-scatter.7
  187.9 23.1 reduce-scatter.9
  213.9 23.0 reduce-scatter.11
  239.4 23.0 reduce-scatter.13
  264.8 53.8 all-gather.19
  320.9 50.5 all-gather.17
  373.6 50.7 all-gather.15
  426.7 50.7 all-gather.13
  479.5 50.7 all-gather.11
